TPU v7x, 64 devices: a 2x2x8 block of a 4x4x8 slice. The times are simulated.
64 devices in a mesh: data: 4 (over x, y), model: 16 (over z, core).
Axes of the slice: x: 2, y: 2, z: 8, core: 2. Of those that a mesh axis runs over, the one named last changes fastest.
The devices are a block of a 4x4x8 slice.
Arguments:
- hidden: bfloat16 [128, 5120], P('data'), parts along dimension 0
- w_head: bfloat16 [5120, 131072], P(None, 'model')
- store_keys: bfloat16 [16384, 5120], P('model')
- store_tok: int32 [16384], P('model')
- range_bounds: int32 [16, 17], P('model')
- temperature: float32 [], replicated
- mix_weight: float32 [], replicated
Outputs:
- output: float32 [128, 131072], P('data', 'model'), parts along dimension 0
There are 4 independent parts. A program takes and returns all parts, laid end to end along the dimension named above; an argument that names none is the same for every part.
All inputs are finite; a program needn't handle non-finite values.
Results may differ from a plain program's by a relative error of at most 0.001.
Values are sent between devices in bfloat16 or wider.
A program may use at most 768 MiB of HBM per device.

v0:
```python
import functools

import jax
import jax.numpy as jnp
from jax import lax
from jax.experimental import pallas as pl
from jax.experimental.pallas import tpu as pltpu
from jax.sharding import PartitionSpec as P

MESH_ID = pl.DeviceIdType.MESH
LANES = 128
BLOCK = 256
SLOTS = 16
F32 = jnp.float32
LOWEST = float(jnp.finfo(jnp.float32).min)
VMEM_BYTES = 64 * 1024 * 1024 - 65536
EXTRA = 16


def lane_groups(x, op):
    x = op(x, pltpu.roll(x, 64, 1))
    return op(x, pltpu.roll(x, 32, 1))


def score_kernel(group, hid_ref, tok_ref, rb_ref, tau_ref, lam_ref, keys_ref, w_ref,
                 gath_out, logit_out, meta_out, scale_out, stat_out,
                 kbuf, wbuf, gath, toks, meta, logits, mrun, srun, stats,
                 ksem, wsem, osem, rs, rr, ls, lr, ps, pr, ss, sr):
    me = lax.axis_index('model')
    chips = group // 2
    chip, core = me // 2, me % 2
    partner = me + 1 - 2 * core
    right = ((chip + 1) % chips) * 2 + core
    left = ((chip + chips - 1) % chips) * 2 + core
    rows, dim = hid_ref.shape
    quarter = kbuf.shape[1]
    half = (quarter + EXTRA) // 2
    width = logits.shape[1]
    blocks = width // BLOCK
    far = chips // 2
    extra = quarter + 8

    barrier = pltpu.get_barrier_semaphore()
    for p in range(1, group):
        pl.semaphore_signal(barrier, inc=1, device_id={'model': (me + p) % group}, device_id_type=MESH_ID)

    def key_copy(c):
        return pltpu.make_async_copy(keys_ref.at[pl.ds(pl.multiple_of(c * quarter, quarter), quarter)],
                                     kbuf.at[c], ksem.at[c])

    def w_copy(i):
        slot = lax.rem(i, SLOTS)
        return pltpu.make_async_copy(w_ref.at[:, pl.ds(pl.multiple_of(i * BLOCK, BLOCK), BLOCK)],
                                     wbuf.at[slot], wsem.at[slot])

    for c in range(4):
        key_copy(c).start()
    for i in range(SLOTS):
        w_copy(i).start()

    mrun[...] = jnp.full(mrun.shape, LOWEST, F32)
    srun[...] = jnp.zeros(srun.shape, F32)
    tok = tok_ref[...].astype(F32)
    gath[me, pl.ds(quarter, 8), :] = tok
    gath[me, pl.ds(extra, 8), :] = jnp.zeros((8, LANES), F32)
    gath[me, pl.ds(extra, 1), 0:rb_ref.shape[1]] = rb_ref[...].astype(F32)
    for h in range(2):
        toks[h * LANES:(h + 1) * LANES, :] = jnp.concatenate(
            [jnp.broadcast_to(tok[2 * k + h:2 * k + h + 1], (rows, LANES)) for k in range(4)], axis=0).T

    lane = lax.broadcasted_iota(jnp.int32, (quarter, LANES), 1)
    gath[me, 0:quarter, :] = jnp.zeros((quarter, LANES), F32)

    def score_step(c, carry):
        key_copy(c).wait()
        norm = jnp.zeros((quarter, LANES), F32)
        for t in range(dim // LANES):
            x = kbuf[c, :, t * LANES:(t + 1) * LANES].astype(F32)
            norm = norm + x * x
        norm = jnp.sum(norm, axis=1, keepdims=True)
        hid4 = jnp.concatenate([hid_ref[...]] * 4, axis=0)
        dot = lax.dot_general(kbuf[c], hid4, (((1,), (1,)), ((), ())), preferred_element_type=F32)
        score = (2.0 * dot - norm) / tau_ref[0]
        score = jnp.where(lane // rows == c, score, gath[me, 0:quarter, :])
        gath[me, 0:quarter, :] = score
        return carry

    lax.fori_loop(0, 4, score_step, 0)

    top = functools.reduce(jnp.maximum, [gath[me, r * 8:r * 8 + 8, :] for r in range(quarter // 8)])
    top = lane_groups(jnp.broadcast_to(jnp.max(top, axis=0, keepdims=True), (8, LANES)), jnp.maximum)
    sub = lax.broadcasted_iota(jnp.int32, (8, LANES), 0)

    def exp_step(r, total):
        at = pl.ds(pl.multiple_of(r * 8, 8), 8)
        e = jnp.exp(gath[me, at, :] - top)
        total = total + e
        ids = toks[at, :]
        last = (ids != pltpu.roll(ids, 7, 0)) | (sub == 7)
        for d in (1, 2, 4):
            same = (ids == pltpu.roll(ids, d, 0)) & (sub >= d)
            e = e + jnp.where(same, pltpu.roll(e, d, 0), 0.0)
        gath[me, at, :] = jnp.where(last, e, 0.0)
        return total

    total = lax.fori_loop(0, quarter // 8, exp_step, jnp.zeros((8, LANES), F32), unroll=8)
    total = lane_groups(jnp.broadcast_to(jnp.sum(total, axis=0, keepdims=True), (8, LANES)), jnp.add)
    gath[me, pl.ds(extra + 1, 1), :] = top[0:1]
    gath[me, pl.ds(extra + 2, 1), :] = total[0:1]

    pl.semaphore_wait(barrier, group - 1)

    def remote(ref, slot, part, send, recv, target):
        view = ref.at[slot] if part is None else ref.at[slot, pl.ds(part * half, half)]
        return pltpu.make_async_remote_copy(view, view, send, recv, device_id={'model': target},
                                            device_id_type=MESH_ID)

    def origin(step, sign):
        return ((chip + chips + sign * step) % chips) * 2 + core

    def right_piece(s, h):
        return remote(gath, origin(s - 1, -1), h, rs.at[2 * s - 2 + h], rr.at[2 * s - 2 + h], right)

    def right_landed(s, h):
        return remote(gath, origin(s, -1), h, rs.at[2 * s - 2 + h], rr.at[2 * s - 2 + h], right)

    def left_piece(s, h):
        return remote(gath, origin(s - 1, 1), h, ls.at[2 * s - 2 + h], lr.at[2 * s - 2 + h], left)

    def left_landed(s, h):
        return remote(gath, origin(s, 1), h, ls.at[2 * s - 2 + h], lr.at[2 * s - 2 + h], left)

    def across(step, h, q):
        return remote(gath, origin(step, -1), h, ps.at[q, h], pr.at[q, h], partner)

    def across_landed(step, h, q):
        slot = origin(step, -1) + 1 - 2 * core
        return remote(gath, slot, h, ps.at[q, h], pr.at[q, h], partner)

    for h in range(2):
        right_piece(1, h).start()
        left_piece(1, h).start()
    for h in range(2):
        across(0, h, 0).start()

    right_order = [(s, h) for s in range(1, far) for h in range(2)] + [(far, 0)]
    left_order = [(s, h) for s in range(1, far) for h in range(2)] + [(far, 1)]

    def ring_event(e):
        s, h = right_order[e]
        right_landed(s, h).wait_recv()
        if (s + 1, h) in right_order:
            right_piece(s + 1, h).start()
        across(s, h, s).start()
        s, h = left_order[e]
        left_landed(s, h).wait_recv()
        if (s + 1, h) in left_order:
            left_piece(s + 1, h).start()
        across(chips - s, h, chips - s).start()

    gath_copy = pltpu.make_async_copy(gath, gath_out, osem.at[0])
    meta_copy = pltpu.make_async_copy(meta, meta_out, osem.at[1])

    def gathered():
        for q in range(chips):
            for h in range(2):
                across_landed(q, h, q).wait_recv()
        gath_copy.start()
        tile_lane = lax.broadcasted_iota(jnp.int32, (8, LANES), 1)
        place = lax.broadcasted_iota(jnp.int32, (8, LANES), 0) * LANES + tile_lane
        high = functools.reduce(jnp.maximum, [gath[g, extra + 1:extra + 2, :] for g in range(group)])
        shares = [jnp.exp(gath[g, extra + 1:extra + 2, :] - high) for g in range(group)]
        whole = sum(gath[g, extra + 2:extra + 3, :] * shares[g] for g in range(group))
        for g in range(group):
            scale_out[g:g + 1, :] = shares[g] * (lam_ref[0] / whole)

        def index_step(g, carry):
            bounds = gath[g, extra:extra + 8, :]
            first = jnp.sum(jnp.where(tile_lane == me, bounds, 0.0), axis=1, keepdims=True)[0:1].astype(jnp.int32)
            after = jnp.sum(jnp.where(tile_lane == me + 1, bounds, 0.0), axis=1, keepdims=True)[0:1].astype(jnp.int32)
            ids = gath[g, quarter:quarter + 8, :].astype(jnp.int32)
            meta[g, 0:8, :] = jnp.where((place >= first) & (place < after), ids - me * width, width)
            meta[g, 8:16, :] = bounds.astype(jnp.int32)
            return carry

        lax.fori_loop(0, group, index_step, 0, unroll=4)
        meta_copy.start()

    def block_stats(i, keep):
        parts = [logits[:, pl.ds(pl.multiple_of(i * BLOCK, BLOCK) + t * LANES, LANES)] for t in range(BLOCK // LANES)]
        old = mrun[...]
        new = functools.reduce(jnp.maximum, parts, old)
        srun[...] = sum((jnp.exp(x - new) for x in parts), srun[...] * jnp.exp(old - new)) * keep
        mrun[...] = new

    bands = 4
    band = width // bands

    def logit_copy(b):
        at = pl.ds(b * band, band)
        return pltpu.make_async_copy(logits.at[:, at], logit_out.at[:, at], osem.at[2 + b])

    logits[:, 0:BLOCK] = jnp.full((rows, BLOCK), LOWEST, F32)

    def w_step(i, carry):
        slot = lax.rem(i, SLOTS)
        w_copy(i).wait()
        block_stats(jnp.maximum(i - 1, 0), jnp.where(i > 0, 1.0, 0.0))
        acc = jnp.dot(hid_ref[...], wbuf[slot], preferred_element_type=F32)
        logits[:, pl.ds(pl.multiple_of(i * BLOCK, BLOCK), BLOCK)] = acc

        @pl.when(i + SLOTS < blocks)
        def _():
            w_copy(i + SLOTS).start()

        for e in range(len(right_order)):
            pl.when(i == 4 + 2 * e)(functools.partial(ring_event, e))
        pl.when(i == 6 + 2 * len(right_order))(gathered)
        for b in range(bands - 1):
            pl.when(i == (b + 1) * (blocks // bands))(logit_copy(b).start)
        return carry

    lax.fori_loop(0, blocks, w_step, 0)
    block_stats(blocks - 1, 1.0)
    logit_copy(bands - 1).start()

    peak = jnp.max(mrun[...], axis=1, keepdims=True)
    tot = jnp.sum(srun[...] * jnp.exp(mrun[...] - peak), axis=1, keepdims=True)
    pad = jnp.zeros((64 - rows, LANES), F32)
    square = jnp.concatenate([jnp.broadcast_to(peak, (rows, LANES)), pad, jnp.broadcast_to(tot, (rows, LANES)), pad],
                             axis=0)
    stats[me] = square.T[0:1]

    def stat_copy(p, slot):
        return remote(stats, slot, None, ss.at[p], sr.at[p], (me + p) % group)

    for p in range(1, group):
        stat_copy(p, me).start()
    for p in range(1, group):
        stat_copy(p, (me + group - p) % group).wait_recv()

    row_lane = lax.broadcasted_iota(jnp.int32, (1, LANES), 1)
    every = [stats[g] for g in range(group)]
    high = functools.reduce(jnp.maximum, every)
    total = jnp.zeros((1, LANES), F32)
    for one in every:
        moved = pltpu.roll(jnp.broadcast_to(one, (8, LANES)), 64, 1)[0:1]
        total = total + moved * jnp.exp(jnp.where(row_lane < rows, one - high, 0.0))
    share = (1.0 - lam_ref[0]) / jnp.where(row_lane < rows, total, 1.0)
    stat_out[0:rows] = jnp.broadcast_to(high, (LANES, LANES)).T[0:rows]
    stat_out[rows:2 * rows] = jnp.broadcast_to(share, (LANES, LANES)).T[0:rows]

    for s, h in right_order:
        right_piece(s, h).wait_send()
    for s, h in left_order:
        left_piece(s, h).wait_send()
    for q in range(chips):
        for h in range(2):
            across(q, h, q).wait_send()
    for p in range(1, group):
        stat_copy(p, me).wait_send()
    gath_copy.wait()
    meta_copy.wait()
    for b in range(bands):
        logit_copy(b).wait()


def mix_kernel(group, meta_hbm, gath_hbm, logit_hbm, scale_ref, stat_ref, out_ref, meta, gath, logits, hist, sems):
    me = lax.axis_index('model')
    rows, width = logits.shape
    copies = [pltpu.make_async_copy(a, b, sems.at[i])
              for i, (a, b) in enumerate(((meta_hbm, meta), (gath_hbm, gath), (logit_hbm, logits)))]
    for c in copies:
        c.start()

    def zero_step(i, carry):
        hist[pl.ds(pl.multiple_of(i * LANES, LANES), LANES), :] = jnp.zeros((LANES, LANES), F32)
        return carry

    lax.fori_loop(0, width // LANES, zero_step, 0)
    hist[width:width + 8, :] = jnp.zeros((8, LANES), F32)
    copies[0].wait()
    copies[1].wait()
    lane = lax.broadcasted_iota(jnp.int32, (1, LANES), 1)

    def source_step(g, carry):
        low, high = meta[g, 8, me], meta[g, 8, me + 1]
        scale = scale_ref[pl.ds(g, 1), :]

        def eight(q, c):
            factor = jnp.where(lane // rows == lax.shift_right_logical(q, 5), scale, 0.0)
            row = jnp.bitwise_and(q, 31) * 8
            at = [meta[g, lax.shift_right_logical(q, 4), jnp.bitwise_and(q, 15) * 8 + s] for s in range(8)]
            new = [hist[pl.ds(at[s], 1), :] + gath[g, pl.ds(row + s, 1), :] * factor for s in range(8)]
            for s in range(8):
                hist[pl.ds(at[s], 1), :] = new[s]
            return c

        lax.fori_loop(lax.shift_right_logical(low, 3), lax.shift_right_logical(high + 7, 3), eight, 0)
        return carry

    lax.fori_loop(0, group, source_step, 0)
    copies[2].wait()
    peak = stat_ref[0:rows]
    share = stat_ref[rows:2 * rows]

    def out_step(i, carry):
        for u in range(8):
            at = pl.ds(pl.multiple_of((i * 8 + u) * LANES, LANES), LANES)
            turned = hist[at, :].T
            knn = (turned[0:rows] + turned[rows:2 * rows]) + (turned[2 * rows:3 * rows] + turned[3 * rows:4 * rows])
            out_ref[:, at] = jnp.log(knn + jnp.exp(logits[:, at] - peak) * share)
        return carry

    lax.fori_loop(0, width // LANES // 8, out_step, 0)


def solution(mesh):
    group = mesh.shape['model']

    def local_step(hidden, w_local, keys_local, tok_local, bounds_local, temperature, mix_weight):
        rows, dim = hidden.shape
        width = w_local.shape[1]
        store = keys_local.shape[0]
        quarter = store // 4
        chips = group // 2
        vmem = pl.BlockSpec(memory_space=pltpu.VMEM)
        smem = pl.BlockSpec(memory_space=pltpu.SMEM)
        hbm = pl.BlockSpec(memory_space=pltpu.HBM)
        dma = pltpu.SemaphoreType.DMA
        gath_shape = (group, quarter + EXTRA, LANES)
        meta_shape = (group, 16, LANES)
        gath, logits, meta, scale, stat = pl.pallas_call(
            functools.partial(score_kernel, group),
            out_shape=(jax.ShapeDtypeStruct(gath_shape, F32), jax.ShapeDtypeStruct((rows, width), F32),
                       jax.ShapeDtypeStruct(meta_shape, jnp.int32), jax.ShapeDtypeStruct((group, LANES), F32),
                       jax.ShapeDtypeStruct((2 * rows, LANES), F32)),
            in_specs=[vmem, vmem, vmem, smem, smem, hbm, hbm],
            out_specs=(hbm, hbm, hbm, vmem, vmem),
            scratch_shapes=[
                pltpu.VMEM((4, quarter, dim), jnp.bfloat16),
                pltpu.VMEM((SLOTS, dim, BLOCK), jnp.bfloat16),
                pltpu.VMEM(gath_shape, F32),
                pltpu.VMEM((quarter, LANES), F32),
                pltpu.VMEM(meta_shape, jnp.int32),
                pltpu.VMEM((rows, width), F32),
                pltpu.VMEM((rows, LANES), F32),
                pltpu.VMEM((rows, LANES), F32),
                pltpu.VMEM((group, 1, LANES), F32),
                dma((4,)), dma((SLOTS,)), dma((6,)),
                dma((chips,)), dma((chips,)), dma((chips,)), dma((chips,)),
                dma((chips, 2)), dma((chips, 2)),
                dma((group,)), dma((group,)),
            ],
            compiler_params=pltpu.CompilerParams(collective_id=0, has_side_effects=True, vmem_limit_bytes=VMEM_BYTES),
            name='score_gather_head',
        )(hidden, tok_local.reshape(store // LANES, LANES), bounds_local, temperature.reshape(1),
          mix_weight.reshape(1), keys_local, w_local)
        return mix_call(group, rows, width, meta, gath, logits, scale, stat)

    return jax.shard_map(local_step, mesh=mesh,
                         in_specs=(P('data', None), P(None, 'model'), P('model', None), P('model'),
                                   P('model', None), P(), P()),
                         out_specs=P('data', 'model'), check_vma=False)


def mix_call(group, rows, width, meta, gath, logits, scale, stat):
    vmem = pl.BlockSpec(memory_space=pltpu.VMEM)
    hbm = pl.BlockSpec(memory_space=pltpu.HBM)
    return pl.pallas_call(
        functools.partial(mix_kernel, group),
        out_shape=jax.ShapeDtypeStruct((rows, width), F32),
        in_specs=[hbm, hbm, hbm, vmem, vmem],
        out_specs=vmem,
        scratch_shapes=[
            pltpu.SMEM(meta.shape, jnp.int32),
            pltpu.VMEM(gath.shape, F32),
            pltpu.VMEM((rows, width), F32),
            pltpu.VMEM((width + 8, LANES), F32),
            pltpu.SemaphoreType.DMA((3,)),
        ],
        compiler_params=pltpu.CompilerParams(vmem_limit_bytes=VMEM_BYTES),
        name='bin_mix',
    )(meta, gath, logits, scale, stat)
```

profile of v0, /device:TPU:21, one launch (start us, length us, event | category | flops | bytes accessed | tf_op | source)
XLA Modules:
  0.0 72.4 jit_solution(10045134981425221691)
XLA Ops:
  1.3 57.4 %score_gather_head.1 = (f32[16,272,128]{2,1,0:T(8,128)}, f32[32,8192]{1,0:T(8,128)}, s32[16,16,128]{2,1,0:T(8,128)}, f32[16,128]{1,0:T(8,128)}, f32[64,128]{1,0:T(8,128)}) custom-call(bf16[32,5120]{1,0:T(8,128)(2,1)} %hid_ref.1, s32[8,128]{1,0:T(8,128)} %bitcast.5, s32[1,17]{1,0:T(1,128)} %rb_ref.1, f32[1]{0:T(128)} %bitcast.3.tau_ref, f32[1]{0:T(128)} %bitcast.4.lam_ref, ...), custom_call_target="tpu_custom_call" | custom-call | tf_op jit(solution)/shard_map/score_gather_head/pallas_call | solution.py:333
  58.7 13.7 %bin_mix.1 = f32[32,8192]{1,0:T(8,128)} custom-call(s32[16,16,128]{2,1,0:T(8,128)} %get-tuple-element.10.meta_hbm, f32[16,272,128]{2,1,0:T(8,128)} %get-tuple-element.11.gath_hbm, f32[32,8192]{1,0:T(8,128)} %get-tuple-element.12.logit_hbm, f32[16,128]{1,0:T(8,128)} %get-tuple-element.13.scale_ref, f32[64,128]{1,0:T(8,128)} %get-tuple-element.14.stat_ref), custom_call_target="tpu_custom_call" | custom-call | tf_op jit(solution)/shard_map/bin_mix/pallas_call | solution.py:370
where the time goes:
time: 73 us; the launch traced here: 72.4 us
  Pallas kernels  71.1 us (97%)
  between operations  1.3 us (2%)
    pallas_call x1, Pallas kernels, local_step(): pl.pallas_call(functools.partial(score_kernel, group), out_shape=(jax.Sha...  57.4 us
    pallas_call x1, Pallas kernels, mix_call(): pl.pallas_call(functools.partial(mix_kernel, group), out_shape=jax.ShapeD...  13.7 us

commit v1 on v0

--- a/solution.py
+++ b/solution.py
@@ -55,9 +55,6 @@
 
     for c in range(4):
         key_copy(c).start()
-    for i in range(SLOTS):
-        w_copy(i).start()
-
     mrun[...] = jnp.full(mrun.shape, LOWEST, F32)
     srun[...] = jnp.zeros(srun.shape, F32)
     tok = tok_ref[...].astype(F32)
@@ -73,6 +70,8 @@
 
     def score_step(c, carry):
         key_copy(c).wait()
+        for u in range(SLOTS // 4):
+            w_copy(c * (SLOTS // 4) + u).start()
         norm = jnp.zeros((quarter, LANES), F32)
         for t in range(dim // LANES):
             x = kbuf[c, :, t * LANES:(t + 1) * LANES].astype(F32)
@@ -214,8 +213,8 @@
             w_copy(i + SLOTS).start()
 
         for e in range(len(right_order)):
-            pl.when(i == 4 + 2 * e)(functools.partial(ring_event, e))
-        pl.when(i == 6 + 2 * len(right_order))(gathered)
+            pl.when(i == 3 + 3 * e)(functools.partial(ring_event, e))
+        pl.when(i == 4 + 3 * len(right_order))(gathered)
         for b in range(bands - 1):
             pl.when(i == (b + 1) * (blocks // bands))(logit_copy(b).start)
         return carry
@@ -265,13 +264,24 @@
         logit_copy(b).wait()
 
 
-def mix_kernel(group, meta_hbm, gath_hbm, logit_hbm, scale_ref, stat_ref, out_ref, meta, gath, logits, hist, sems):
+def mix_kernel(group, meta_hbm, gath_hbm, logit_hbm, scale_ref, stat_ref, out_hbm,
+               meta, gath, logits, hist, sems, gsem, osem):
     me = lax.axis_index('model')
     rows, width = logits.shape
-    copies = [pltpu.make_async_copy(a, b, sems.at[i])
-              for i, (a, b) in enumerate(((meta_hbm, meta), (gath_hbm, gath), (logit_hbm, logits)))]
-    for c in copies:
-        c.start()
+    span = meta.shape[0] // group
+    bounds = span // 2
+    bands = osem.shape[0]
+    band = width // bands
+    meta_copy = pltpu.make_async_copy(meta_hbm, meta, sems.at[0])
+    logit_copy = pltpu.make_async_copy(logit_hbm, logits, sems.at[1])
+
+    def gath_copy(g):
+        return pltpu.make_async_copy(gath_hbm.at[g], gath.at[g], gsem.at[g])
+
+    meta_copy.start()
+    for g in range(group):
+        gath_copy(g).start()
+    logit_copy.start()
 
     def zero_step(i, carry):
         hist[pl.ds(pl.multiple_of(i * LANES, LANES), LANES), :] = jnp.zeros((LANES, LANES), F32)
@@ -279,18 +289,20 @@
 
     lax.fori_loop(0, width // LANES, zero_step, 0)
     hist[width:width + 8, :] = jnp.zeros((8, LANES), F32)
-    copies[0].wait()
-    copies[1].wait()
+    meta_copy.wait()
     lane = lax.broadcasted_iota(jnp.int32, (1, LANES), 1)
 
     def source_step(g, carry):
-        low, high = meta[g, 8, me], meta[g, 8, me + 1]
+        start = g * span
+        low, high = meta[start + bounds + me], meta[start + bounds + me + 1]
         scale = scale_ref[pl.ds(g, 1), :]
+        gath_copy(g).wait()
 
         def eight(q, c):
             factor = jnp.where(lane // rows == lax.shift_right_logical(q, 5), scale, 0.0)
             row = jnp.bitwise_and(q, 31) * 8
-            at = [meta[g, lax.shift_right_logical(q, 4), jnp.bitwise_and(q, 15) * 8 + s] for s in range(8)]
+            first = start + q * 8
+            at = [meta[first + s] for s in range(8)]
             new = [hist[pl.ds(at[s], 1), :] + gath[g, pl.ds(row + s, 1), :] * factor for s in range(8)]
             for s in range(8):
                 hist[pl.ds(at[s], 1), :] = new[s]
@@ -300,19 +312,27 @@
         return carry
 
     lax.fori_loop(0, group, source_step, 0)
-    copies[2].wait()
+    logit_copy.wait()
     peak = stat_ref[0:rows]
     share = stat_ref[rows:2 * rows]
+    steps = 8
+
+    def out_copy(b):
+        at = pl.ds(pl.multiple_of(b * band, band), band)
+        return pltpu.make_async_copy(logits.at[:, at], out_hbm.at[:, at], osem.at[b])
 
     def out_step(i, carry):
-        for u in range(8):
-            at = pl.ds(pl.multiple_of((i * 8 + u) * LANES, LANES), LANES)
+        for u in range(steps):
+            at = pl.ds(pl.multiple_of(i * band + u * LANES, LANES), LANES)
             turned = hist[at, :].T
             knn = (turned[0:rows] + turned[rows:2 * rows]) + (turned[2 * rows:3 * rows] + turned[3 * rows:4 * rows])
-            out_ref[:, at] = jnp.log(knn + jnp.exp(logits[:, at] - peak) * share)
+            logits[:, at] = jnp.log(knn + jnp.exp(logits[:, at] - peak) * share)
+        out_copy(i).start()
         return carry
 
-    lax.fori_loop(0, width // LANES // 8, out_step, 0)
+    lax.fori_loop(0, bands, out_step, 0)
+    for b in range(bands):
+        out_copy(b).wait()
 
 
 def solution(mesh):
@@ -367,18 +387,19 @@
 def mix_call(group, rows, width, meta, gath, logits, scale, stat):
     vmem = pl.BlockSpec(memory_space=pltpu.VMEM)
     hbm = pl.BlockSpec(memory_space=pltpu.HBM)
+    dma = pltpu.SemaphoreType.DMA
     return pl.pallas_call(
         functools.partial(mix_kernel, group),
         out_shape=jax.ShapeDtypeStruct((rows, width), F32),
         in_specs=[hbm, hbm, hbm, vmem, vmem],
-        out_specs=vmem,
+        out_specs=hbm,
         scratch_shapes=[
-            pltpu.SMEM(meta.shape, jnp.int32),
+            pltpu.SMEM((meta.size,), jnp.int32),
             pltpu.VMEM(gath.shape, F32),
             pltpu.VMEM((rows, width), F32),
             pltpu.VMEM((width + 8, LANES), F32),
-            pltpu.SemaphoreType.DMA((3,)),
+            dma((2,)), dma((group,)), dma((width // (8 * LANES),)),
         ],
         compiler_params=pltpu.CompilerParams(vmem_limit_bytes=VMEM_BYTES),
         name='bin_mix',
-    )(meta, gath, logits, scale, stat)
+    )(meta.reshape(meta.size), gath, logits, scale, stat)

time: 73 us -> 56.7 us (0.78)
  Pallas kernels: 71.1 us -> 55.1 us
    pallas_call x1, Pallas kernels: 57.4 us -> 44 us  [local_step(): pl.pallas_call(functools.partial(score_kernel, group), out_shape=(jax.Sha...]
    pallas_call x1, Pallas kernels: 13.7 us -> 11.1 us  [mix_call(): pl.pallas_call(functools.partial(mix_kernel, group), out_shape=jax.ShapeD...]
where the time goes in v1:
time: 56.7 us; the launch traced here: 56.4 us
  Pallas kernels  55.1 us (97%)
  between operations  1.3 us (2%)
    pallas_call x1, Pallas kernels, local_step(): pl.pallas_call(functools.partial(score_kernel, group), out_shape=(jax.Sha...  44 us
    pallas_call x1, Pallas kernels, mix_call(): pl.pallas_call(functools.partial(mix_kernel, group), out_shape=jax.ShapeD...  11.1 us

profile of v1, /device:TPU:21, one launch (start us, length us, event | category | flops | bytes accessed | tf_op | source)
XLA Modules:
  0.0 56.4 jit_solution(17893518675637843306)
XLA Ops:
  1.3 44.0 %score_gather_head.1 = (f32[16,272,128]{2,1,0:T(8,128)}, f32[32,8192]{1,0:T(8,128)}, s32[16,16,128]{2,1,0:T(8,128)}, f32[16,128]{1,0:T(8,128)}, f32[64,128]{1,0:T(8,128)}) custom-call(bf16[32,5120]{1,0:T(8,128)(2,1)} %hid_ref.1, s32[8,128]{1,0:T(8,128)} %bitcast.7, s32[1,17]{1,0:T(1,128)} %rb_ref.1, f32[1]{0:T(128)} %bitcast.4.tau_ref, f32[1]{0:T(128)} %bitcast.5.lam_ref, ...), custom_call_target="tpu_custom_call" | custom-call | tf_op jit(solution)/shard_map/score_gather_head/pallas_call | solution.py:353
  45.3 11.1 %bin_mix.1 = f32[32,8192]{1,0:T(8,128)} custom-call(s32[32768]{0:T(1024)} %bitcast.6, f32[16,272,128]{2,1,0:T(8,128)} %get-tuple-element.11.gath_hbm, f32[32,8192]{1,0:T(8,128)} %get-tuple-element.12.logit_hbm, f32[16,128]{1,0:T(8,128)} %get-tuple-element.13.scale_ref, f32[64,128]{1,0:T(8,128)} %get-tuple-element.14.stat_ref), custom_call_target="tpu_custom_call" | custom-call | tf_op jit(solution)/shard_map/bin_mix/pallas_call | solution.py:391

commit v2 on v1

--- a/solution.py
+++ b/solution.py
@@ -10,7 +10,8 @@
 MESH_ID = pl.DeviceIdType.MESH
 LANES = 128
 BLOCK = 256
-SLOTS = 16
+SLOTS = 14
+GROUP = 16
 F32 = jnp.float32
 LOWEST = float(jnp.finfo(jnp.float32).min)
 VMEM_BYTES = 64 * 1024 * 1024 - 65536
@@ -24,7 +25,7 @@
 
 def score_kernel(group, hid_ref, tok_ref, rb_ref, tau_ref, lam_ref, keys_ref, w_ref,
                  gath_out, logit_out, meta_out, scale_out, stat_out,
-                 kbuf, wbuf, gath, toks, meta, logits, mrun, srun, stats,
+                 kbuf, wbuf, gath, logits, toks, meta, mrun, srun, stats,
                  ksem, wsem, osem, rs, rr, ls, lr, ps, pr, ss, sr):
     me = lax.axis_index('model')
     chips = group // 2
@@ -70,8 +71,8 @@
 
     def score_step(c, carry):
         key_copy(c).wait()
-        for u in range(SLOTS // 4):
-            w_copy(c * (SLOTS // 4) + u).start()
+        for u in range(3):
+            w_copy(3 * c + u).start()
         norm = jnp.zeros((quarter, LANES), F32)
         for t in range(dim // LANES):
             x = kbuf[c, :, t * LANES:(t + 1) * LANES].astype(F32)
@@ -85,24 +86,31 @@
         return carry
 
     lax.fori_loop(0, 4, score_step, 0)
+    for i in range(12, SLOTS):
+        w_copy(i).start()
 
     top = functools.reduce(jnp.maximum, [gath[me, r * 8:r * 8 + 8, :] for r in range(quarter // 8)])
     top = lane_groups(jnp.broadcast_to(jnp.max(top, axis=0, keepdims=True), (8, LANES)), jnp.maximum)
     sub = lax.broadcasted_iota(jnp.int32, (8, LANES), 0)
 
+    def run_sums(e, ids):
+        for d in (1, 2, 4):
+            e = e + jnp.where((ids == pltpu.roll(ids, d, 0)) & (sub >= d), pltpu.roll(e, d, 0), 0.0)
+        return e
+
     def exp_step(r, total):
-        at = pl.ds(pl.multiple_of(r * 8, 8), 8)
-        e = jnp.exp(gath[me, at, :] - top)
-        total = total + e
-        ids = toks[at, :]
-        last = (ids != pltpu.roll(ids, 7, 0)) | (sub == 7)
-        for d in (1, 2, 4):
-            same = (ids == pltpu.roll(ids, d, 0)) & (sub >= d)
-            e = e + jnp.where(same, pltpu.roll(e, d, 0), 0.0)
-        gath[me, at, :] = jnp.where(last, e, 0.0)
-        return total
-
-    total = lax.fori_loop(0, quarter // 8, exp_step, jnp.zeros((8, LANES), F32), unroll=8)
+        at = [pl.ds(pl.multiple_of(r * GROUP + 8 * u, 8), 8) for u in range(2)]
+        e = [jnp.exp(gath[me, a, :] - top) for a in at]
+        ids = [toks[a, :] for a in at]
+        sums = [run_sums(e[u], ids[u]) for u in range(2)]
+        spread = lambda x: jnp.broadcast_to(x, (8, LANES))
+        sums[1] = sums[1] + jnp.where(ids[1] == spread(ids[0][7:8]), spread(sums[0][7:8]), 0.0)
+        after = jnp.where(sub == 7, spread(ids[1][0:1]), pltpu.roll(ids[0], 7, 0))
+        gath[me, at[0], :] = jnp.where(ids[0] != after, sums[0], 0.0)
+        gath[me, at[1], :] = jnp.where((ids[1] != pltpu.roll(ids[1], 7, 0)) | (sub == 7), sums[1], 0.0)
+        return total + (e[0] + e[1])
+
+    total = lax.fori_loop(0, quarter // GROUP, exp_step, jnp.zeros((8, LANES), F32), unroll=4)
     total = lane_groups(jnp.broadcast_to(jnp.sum(total, axis=0, keepdims=True), (8, LANES)), jnp.add)
     gath[me, pl.ds(extra + 1, 1), :] = top[0:1]
     gath[me, pl.ds(extra + 2, 1), :] = total[0:1]
@@ -157,8 +165,8 @@
             left_piece(s + 1, h).start()
         across(chips - s, h, chips - s).start()
 
-    gath_copy = pltpu.make_async_copy(gath, gath_out, osem.at[0])
-    meta_copy = pltpu.make_async_copy(meta, meta_out, osem.at[1])
+    meta_copy = pltpu.make_async_copy(meta, meta_out, osem.at[0])
+    gath_copy = pltpu.make_async_copy(gath, gath_out, osem.at[1])
 
     def gathered():
         for q in range(chips):
@@ -178,11 +186,13 @@
             first = jnp.sum(jnp.where(tile_lane == me, bounds, 0.0), axis=1, keepdims=True)[0:1].astype(jnp.int32)
             after = jnp.sum(jnp.where(tile_lane == me + 1, bounds, 0.0), axis=1, keepdims=True)[0:1].astype(jnp.int32)
             ids = gath[g, quarter:quarter + 8, :].astype(jnp.int32)
-            meta[g, 0:8, :] = jnp.where((place >= first) & (place < after), ids - me * width, width)
-            meta[g, 8:16, :] = bounds.astype(jnp.int32)
+            meta[pl.ds(pl.multiple_of(8 * g, 8), 8), :] = jnp.where((place >= first) & (place < after),
+                                                                    ids - me * width, width)
             return carry
 
         lax.fori_loop(0, group, index_step, 0, unroll=4)
+        for g in range(group):
+            meta[8 * group + g:8 * group + g + 1, :] = gath[g, extra:extra + 1, :].astype(jnp.int32)
         meta_copy.start()
 
     def block_stats(i, keep):
@@ -258,8 +268,8 @@
             across(q, h, q).wait_send()
     for p in range(1, group):
         stat_copy(p, me).wait_send()
+    meta_copy.wait()
     gath_copy.wait()
-    meta_copy.wait()
     for b in range(bands):
         logit_copy(b).wait()
 
@@ -268,8 +278,7 @@
                meta, gath, logits, hist, sems, gsem, osem):
     me = lax.axis_index('model')
     rows, width = logits.shape
-    span = meta.shape[0] // group
-    bounds = span // 2
+    span = meta.shape[0] // (group * 9) * 8
     bands = osem.shape[0]
     band = width // bands
     meta_copy = pltpu.make_async_copy(meta_hbm, meta, sems.at[0])
@@ -294,21 +303,25 @@
 
     def source_step(g, carry):
         start = g * span
-        low, high = meta[start + bounds + me], meta[start + bounds + me + 1]
+        edge = group * span + g * LANES + me
+        low, high = meta[edge], meta[edge + 1]
         scale = scale_ref[pl.ds(g, 1), :]
+
         gath_copy(g).wait()
-
-        def eight(q, c):
-            factor = jnp.where(lane // rows == lax.shift_right_logical(q, 5), scale, 0.0)
-            row = jnp.bitwise_and(q, 31) * 8
-            first = start + q * 8
-            at = [meta[first + s] for s in range(8)]
-            new = [hist[pl.ds(at[s], 1), :] + gath[g, pl.ds(row + s, 1), :] * factor for s in range(8)]
-            for s in range(8):
+        begin, end = lax.shift_right_logical(low, 4), lax.shift_right_logical(high + GROUP - 1, 4)
+
+        def table_rows(q):
+            return tuple(meta[start + q * GROUP + s] for s in range(GROUP))
+
+        def bin_step(q, at):
+            factor = jnp.where(lane // rows == lax.shift_right_logical(q, 4), scale, 0.0)
+            row = jnp.bitwise_and(q, 15) * GROUP
+            new = [hist[pl.ds(at[s], 1), :] + gath[g, pl.ds(row + s, 1), :] * factor for s in range(GROUP)]
+            for s in range(GROUP):
                 hist[pl.ds(at[s], 1), :] = new[s]
-            return c
-
-        lax.fori_loop(lax.shift_right_logical(low, 3), lax.shift_right_logical(high + 7, 3), eight, 0)
+            return table_rows(q + 1)
+
+        lax.fori_loop(begin, end, bin_step, table_rows(begin))
         return carry
 
     lax.fori_loop(0, group, source_step, 0)
@@ -349,7 +362,7 @@
         hbm = pl.BlockSpec(memory_space=pltpu.HBM)
         dma = pltpu.SemaphoreType.DMA
         gath_shape = (group, quarter + EXTRA, LANES)
-        meta_shape = (group, 16, LANES)
+        meta_shape = (group * 9, LANES)
         gath, logits, meta, scale, stat = pl.pallas_call(
             functools.partial(score_kernel, group),
             out_shape=(jax.ShapeDtypeStruct(gath_shape, F32), jax.ShapeDtypeStruct((rows, width), F32),
@@ -361,9 +374,9 @@
                 pltpu.VMEM((4, quarter, dim), jnp.bfloat16),
                 pltpu.VMEM((SLOTS, dim, BLOCK), jnp.bfloat16),
                 pltpu.VMEM(gath_shape, F32),
+                pltpu.VMEM((rows, width), F32),
                 pltpu.VMEM((quarter, LANES), F32),
                 pltpu.VMEM(meta_shape, jnp.int32),
-                pltpu.VMEM((rows, width), F32),
                 pltpu.VMEM((rows, LANES), F32),
                 pltpu.VMEM((rows, LANES), F32),
                 pltpu.VMEM((group, 1, LANES), F32),

time: 56.7 us -> 55.4 us (0.977)
  Pallas kernels: 55.1 us -> 53.6 us
    pallas_call x1, Pallas kernels: 11.1 us -> 9.59 us  [mix_call(): pl.pallas_call(functools.partial(mix_kernel, group), out_shape=jax.ShapeD...]
where the time goes in v2:
time: 55.4 us; the launch traced here: 54.9 us
  Pallas kernels  53.6 us (97%)
  between operations  1.3 us (2%)
    pallas_call x1, Pallas kernels, local_step(): pl.pallas_call(functools.partial(score_kernel, group), out_shape=(jax.Sha...  44 us
    pallas_call x1, Pallas kernels, mix_call(): pl.pallas_call(functools.partial(mix_kernel, group), out_shape=jax.ShapeD...  9.59 us

profile of v2, /device:TPU:21, one launch (start us, length us, event | category | flops | bytes accessed | tf_op | source)
XLA Modules:
  0.0 54.9 jit_solution(3682155615461067607)
XLA Ops:
  1.3 44.0 %score_gather_head.1 = (f32[16,272,128]{2,1,0:T(8,128)}, f32[32,8192]{1,0:T(8,128)}, s32[144,128]{1,0:T(8,128)}, f32[16,128]{1,0:T(8,128)}, f32[64,128]{1,0:T(8,128)}) custom-call(bf16[32,5120]{1,0:T(8,128)(2,1)} %hid_ref.1, s32[8,128]{1,0:T(8,128)} %bitcast.7, s32[1,17]{1,0:T(1,128)} %rb_ref.1, f32[1]{0:T(128)} %bitcast.4.tau_ref, f32[1]{0:T(128)} %bitcast.5.lam_ref, ...), custom_call_target="tpu_custom_call" | custom-call | tf_op jit(solution)/shard_map/score_gather_head/pallas_call | solution.py:366
  45.3 9.6 %bin_mix.1 = f32[32,8192]{1,0:T(8,128)} custom-call(s32[18432]{0:T(1024)} %bitcast.6, f32[16,272,128]{2,1,0:T(8,128)} %get-tuple-element.11.gath_hbm, f32[32,8192]{1,0:T(8,128)} %get-tuple-element.12.logit_hbm, f32[16,128]{1,0:T(8,128)} %get-tuple-element.13.scale_ref, f32[64,128]{1,0:T(8,128)} %get-tuple-element.14.stat_ref), custom_call_target="tpu_custom_call" | custom-call | tf_op jit(solution)/shard_map/bin_mix/pallas_call | solution.py:404

commit v3 on v2

--- a/solution.py
+++ b/solution.py
@@ -23,10 +23,10 @@
     return op(x, pltpu.roll(x, 32, 1))
 
 
-def score_kernel(group, hid_ref, tok_ref, rb_ref, tau_ref, lam_ref, keys_ref, w_ref,
-                 gath_out, logit_out, meta_out, scale_out, stat_out,
-                 kbuf, wbuf, gath, logits, toks, meta, mrun, srun, stats,
-                 ksem, wsem, osem, rs, rr, ls, lr, ps, pr, ss, sr):
+def score_kernel(group, tau_ref, lam_ref, hid_hbm, tok_hbm, rb_hbm, keys_ref, w_ref,
+                 gath_out, logit_out, meta_out, scale_hbm, stat_hbm,
+                 hid_ref, tok_ref, rb_ref, scale_out, stat_out, kbuf, wbuf, gath, logits, toks, meta, mrun, srun, stats,
+                 isem, ksem, wsem, osem, rs, rr, ls, lr, ps, pr, ss, sr):
     me = lax.axis_index('model')
     chips = group // 2
     chip, core = me // 2, me % 2
@@ -41,10 +41,6 @@
     far = chips // 2
     extra = quarter + 8
 
-    barrier = pltpu.get_barrier_semaphore()
-    for p in range(1, group):
-        pl.semaphore_signal(barrier, inc=1, device_id={'model': (me + p) % group}, device_id_type=MESH_ID)
-
     def key_copy(c):
         return pltpu.make_async_copy(keys_ref.at[pl.ds(pl.multiple_of(c * quarter, quarter), quarter)],
                                      kbuf.at[c], ksem.at[c])
@@ -54,10 +50,21 @@
         return pltpu.make_async_copy(w_ref.at[:, pl.ds(pl.multiple_of(i * BLOCK, BLOCK), BLOCK)],
                                      wbuf.at[slot], wsem.at[slot])
 
+    small = [pltpu.make_async_copy(a, b, isem.at[i])
+             for i, (a, b) in enumerate(((hid_hbm, hid_ref), (tok_hbm, tok_ref), (rb_hbm, rb_ref)))]
+    for copy in small:
+        copy.start()
     for c in range(4):
         key_copy(c).start()
+
+    barrier = pltpu.get_barrier_semaphore()
+    for p in range(1, group):
+        pl.semaphore_signal(barrier, inc=1, device_id={'model': (me + p) % group}, device_id_type=MESH_ID)
+
     mrun[...] = jnp.full(mrun.shape, LOWEST, F32)
     srun[...] = jnp.zeros(srun.shape, F32)
+    for copy in small:
+        copy.wait()
     tok = tok_ref[...].astype(F32)
     gath[me, pl.ds(quarter, 8), :] = tok
     gath[me, pl.ds(extra, 8), :] = jnp.zeros((8, LANES), F32)
@@ -167,6 +174,8 @@
 
     meta_copy = pltpu.make_async_copy(meta, meta_out, osem.at[0])
     gath_copy = pltpu.make_async_copy(gath, gath_out, osem.at[1])
+    scale_copy = pltpu.make_async_copy(scale_out, scale_hbm, osem.at[6])
+    stat_copy_out = pltpu.make_async_copy(stat_out, stat_hbm, osem.at[7])
 
     def gathered():
         for q in range(chips):
@@ -181,6 +190,8 @@
         for g in range(group):
             scale_out[g:g + 1, :] = shares[g] * (lam_ref[0] / whole)
 
+        scale_copy.start()
+
         def index_step(g, carry):
             bounds = gath[g, extra:extra + 8, :]
             first = jnp.sum(jnp.where(tile_lane == me, bounds, 0.0), axis=1, keepdims=True)[0:1].astype(jnp.int32)
@@ -258,6 +269,7 @@
     share = (1.0 - lam_ref[0]) / jnp.where(row_lane < rows, total, 1.0)
     stat_out[0:rows] = jnp.broadcast_to(high, (LANES, LANES)).T[0:rows]
     stat_out[rows:2 * rows] = jnp.broadcast_to(share, (LANES, LANES)).T[0:rows]
+    stat_copy_out.start()
 
     for s, h in right_order:
         right_piece(s, h).wait_send()
@@ -270,12 +282,14 @@
         stat_copy(p, me).wait_send()
     meta_copy.wait()
     gath_copy.wait()
+    scale_copy.wait()
+    stat_copy_out.wait()
     for b in range(bands):
         logit_copy(b).wait()
 
 
-def mix_kernel(group, meta_hbm, gath_hbm, logit_hbm, scale_ref, stat_ref, out_hbm,
-               meta, gath, logits, hist, sems, gsem, osem):
+def mix_kernel(group, meta_hbm, gath_hbm, logit_hbm, scale_hbm, stat_hbm, out_hbm,
+               meta, gath, logits, scale_ref, stat_ref, hist, sems, gsem, osem):
     me = lax.axis_index('model')
     rows, width = logits.shape
     span = meta.shape[0] // (group * 9) * 8
@@ -283,14 +297,18 @@
     band = width // bands
     meta_copy = pltpu.make_async_copy(meta_hbm, meta, sems.at[0])
     logit_copy = pltpu.make_async_copy(logit_hbm, logits, sems.at[1])
+    scale_copy = pltpu.make_async_copy(scale_hbm, scale_ref, sems.at[2])
+    stat_copy = pltpu.make_async_copy(stat_hbm, stat_ref, sems.at[3])
 
     def gath_copy(g):
         return pltpu.make_async_copy(gath_hbm.at[g], gath.at[g], gsem.at[g])
 
     meta_copy.start()
+    scale_copy.start()
     for g in range(group):
         gath_copy(g).start()
     logit_copy.start()
+    stat_copy.start()
 
     def zero_step(i, carry):
         hist[pl.ds(pl.multiple_of(i * LANES, LANES), LANES), :] = jnp.zeros((LANES, LANES), F32)
@@ -299,6 +317,7 @@
     lax.fori_loop(0, width // LANES, zero_step, 0)
     hist[width:width + 8, :] = jnp.zeros((8, LANES), F32)
     meta_copy.wait()
+    scale_copy.wait()
     lane = lax.broadcasted_iota(jnp.int32, (1, LANES), 1)
 
     def source_step(g, carry):
@@ -326,6 +345,7 @@
 
     lax.fori_loop(0, group, source_step, 0)
     logit_copy.wait()
+    stat_copy.wait()
     peak = stat_ref[0:rows]
     share = stat_ref[rows:2 * rows]
     steps = 8
@@ -357,7 +377,6 @@
         store = keys_local.shape[0]
         quarter = store // 4
         chips = group // 2
-        vmem = pl.BlockSpec(memory_space=pltpu.VMEM)
         smem = pl.BlockSpec(memory_space=pltpu.SMEM)
         hbm = pl.BlockSpec(memory_space=pltpu.HBM)
         dma = pltpu.SemaphoreType.DMA
@@ -368,9 +387,14 @@
             out_shape=(jax.ShapeDtypeStruct(gath_shape, F32), jax.ShapeDtypeStruct((rows, width), F32),
                        jax.ShapeDtypeStruct(meta_shape, jnp.int32), jax.ShapeDtypeStruct((group, LANES), F32),
                        jax.ShapeDtypeStruct((2 * rows, LANES), F32)),
-            in_specs=[vmem, vmem, vmem, smem, smem, hbm, hbm],
-            out_specs=(hbm, hbm, hbm, vmem, vmem),
+            in_specs=[smem, smem, hbm, hbm, hbm, hbm, hbm],
+            out_specs=(hbm, hbm, hbm, hbm, hbm),
             scratch_shapes=[
+                pltpu.VMEM((rows, dim), jnp.bfloat16),
+                pltpu.VMEM((store // LANES, LANES), jnp.int32),
+                pltpu.VMEM(bounds_local.shape, jnp.int32),
+                pltpu.VMEM((group, LANES), F32),
+                pltpu.VMEM((2 * rows, LANES), F32),
                 pltpu.VMEM((4, quarter, dim), jnp.bfloat16),
                 pltpu.VMEM((SLOTS, dim, BLOCK), jnp.bfloat16),
                 pltpu.VMEM(gath_shape, F32),
@@ -380,15 +404,15 @@
                 pltpu.VMEM((rows, LANES), F32),
                 pltpu.VMEM((rows, LANES), F32),
                 pltpu.VMEM((group, 1, LANES), F32),
-                dma((4,)), dma((SLOTS,)), dma((6,)),
+                dma((3,)), dma((4,)), dma((SLOTS,)), dma((8,)),
                 dma((chips,)), dma((chips,)), dma((chips,)), dma((chips,)),
                 dma((chips, 2)), dma((chips, 2)),
                 dma((group,)), dma((group,)),
             ],
             compiler_params=pltpu.CompilerParams(collective_id=0, has_side_effects=True, vmem_limit_bytes=VMEM_BYTES),
             name='score_gather_head',
-        )(hidden, tok_local.reshape(store // LANES, LANES), bounds_local, temperature.reshape(1),
-          mix_weight.reshape(1), keys_local, w_local)
+        )(temperature.reshape(1), mix_weight.reshape(1), hidden, tok_local.reshape(store // LANES, LANES), bounds_local,
+          keys_local, w_local)
         return mix_call(group, rows, width, meta, gath, logits, scale, stat)
 
     return jax.shard_map(local_step, mesh=mesh,
@@ -398,20 +422,21 @@
 
 
 def mix_call(group, rows, width, meta, gath, logits, scale, stat):
-    vmem = pl.BlockSpec(memory_space=pltpu.VMEM)
     hbm = pl.BlockSpec(memory_space=pltpu.HBM)
     dma = pltpu.SemaphoreType.DMA
     return pl.pallas_call(
         functools.partial(mix_kernel, group),
         out_shape=jax.ShapeDtypeStruct((rows, width), F32),
-        in_specs=[hbm, hbm, hbm, vmem, vmem],
+        in_specs=[hbm] * 5,
         out_specs=hbm,
         scratch_shapes=[
             pltpu.SMEM((meta.size,), jnp.int32),
             pltpu.VMEM(gath.shape, F32),
             pltpu.VMEM((rows, width), F32),
+            pltpu.VMEM(scale.shape, F32),
+            pltpu.VMEM(stat.shape, F32),
             pltpu.VMEM((width + 8, LANES), F32),
-            dma((2,)), dma((group,)), dma((width // (8 * LANES),)),
+            dma((4,)), dma((group,)), dma((width // (8 * LANES),)),
         ],
         compiler_params=pltpu.CompilerParams(vmem_limit_bytes=VMEM_BYTES),
         name='bin_mix',

time: 55.4 us -> 54.8 us (0.989)
  Pallas kernels: 53.6 us -> 53 us
    pallas_call x1, Pallas kernels: 9.59 us -> 8.55 us  [mix_call(): pl.pallas_call(functools.partial(mix_kernel, group), out_shape=jax.ShapeD...]
where the time goes in v3:
time: 54.8 us; the launch traced here: 54.3 us
  Pallas kernels  53 us (97%)
  between operations  1.3 us (2%)
    pallas_call x1, Pallas kernels, local_step(): pl.pallas_call(functools.partial(score_kernel, group), out_shape=(jax.Sha...  44.4 us
    pallas_call x1, Pallas kernels, mix_call(): pl.pallas_call(functools.partial(mix_kernel, group), out_shape=jax.ShapeD...  8.55 us

profile of v3, /device:TPU:21, one launch (start us, length us, event | category | flops | bytes accessed | tf_op | source)
XLA Modules:
  0.0 54.3 jit_solution(11248873632094374766)
XLA Ops:
  1.3 44.4 %score_gather_head.1 = (f32[16,272,128]{2,1,0:T(8,128)}, f32[32,8192]{1,0:T(8,128)}, s32[144,128]{1,0:T(8,128)}, f32[16,128]{1,0:T(8,128)}, f32[64,128]{1,0:T(8,128)}) custom-call(f32[1]{0:T(128)} %bitcast.4.tau_ref, f32[1]{0:T(128)} %bitcast.5.lam_ref, bf16[32,5120]{1,0:T(8,128)(2,1)} %hid_hbm.1, s32[8,128]{1,0:T(8,128)} %bitcast.7, s32[1,17]{1,0:T(1,128)} %rb_hbm.1, ...), custom_call_target="tpu_custom_call" | custom-call | tf_op jit(solution)/shard_map/score_gather_head/pallas_call | solution.py:385
  45.7 8.6 %bin_mix.1 = f32[32,8192]{1,0:T(8,128)} custom-call(s32[18432]{0:T(1024)} %bitcast.6, f32[16,272,128]{2,1,0:T(8,128)} %get-tuple-element.11.gath_hbm, f32[32,8192]{1,0:T(8,128)} %get-tuple-element.12.logit_hbm, f32[16,128]{1,0:T(8,128)} %get-tuple-element.13.scale_hbm, f32[64,128]{1,0:T(8,128)} %get-tuple-element.14.stat_hbm), custom_call_target="tpu_custom_call" | custom-call | tf_op jit(solution)/shard_map/bin_mix/pallas_call | solution.py:427

commit v4 on v3

--- a/solution.py
+++ b/solution.py
@@ -234,8 +234,8 @@
             w_copy(i + SLOTS).start()
 
         for e in range(len(right_order)):
-            pl.when(i == 3 + 3 * e)(functools.partial(ring_event, e))
-        pl.when(i == 4 + 3 * len(right_order))(gathered)
+            pl.when(i == 6 + 3 * e)(functools.partial(ring_event, e))
+        pl.when(i == 7 + 3 * len(right_order))(gathered)
         for b in range(bands - 1):
             pl.when(i == (b + 1) * (blocks // bands))(logit_copy(b).start)
         return carry
@@ -348,7 +348,7 @@
     stat_copy.wait()
     peak = stat_ref[0:rows]
     share = stat_ref[rows:2 * rows]
-    steps = 8
+    steps = band // LANES
 
     def out_copy(b):
         at = pl.ds(pl.multiple_of(b * band, band), band)
@@ -436,7 +436,7 @@
             pltpu.VMEM(scale.shape, F32),
             pltpu.VMEM(stat.shape, F32),
             pltpu.VMEM((width + 8, LANES), F32),
-            dma((4,)), dma((group,)), dma((width // (8 * LANES),)),
+            dma((4,)), dma((group,)), dma((width // (16 * LANES),)),
         ],
         compiler_params=pltpu.CompilerParams(vmem_limit_bytes=VMEM_BYTES),
         name='bin_mix',

time: 54.8 us -> 53.4 us (0.974)
  Pallas kernels: 53 us -> 51.6 us
    pallas_call x1, Pallas kernels: 44.4 us -> 43.6 us  [local_step(): pl.pallas_call(functools.partial(score_kernel, group), out_shape=(jax.Sha...]
where the time goes in v4:
time: 53.4 us; the launch traced here: 52.9 us
  Pallas kernels  51.6 us (97%)
  between operations  1.3 us (2%)
    pallas_call x1, Pallas kernels, local_step(): pl.pallas_call(functools.partial(score_kernel, group), out_shape=(jax.Sha...  43.6 us
    pallas_call x1, Pallas kernels, mix_call(): pl.pallas_call(functools.partial(mix_kernel, group), out_shape=jax.ShapeD...  8.02 us

profile of v4, /device:TPU:21, one launch (start us, length us, event | category | flops | bytes accessed | tf_op | source)
XLA Modules:
  0.0 52.9 jit_solution(853467370989089531)
XLA Ops:
  1.3 43.6 %score_gather_head.1 = (f32[16,272,128]{2,1,0:T(8,128)}, f32[32,8192]{1,0:T(8,128)}, s32[144,128]{1,0:T(8,128)}, f32[16,128]{1,0:T(8,128)}, f32[64,128]{1,0:T(8,128)}) custom-call(f32[1]{0:T(128)} %bitcast.4.tau_ref, f32[1]{0:T(128)} %bitcast.5.lam_ref, bf16[32,5120]{1,0:T(8,128)(2,1)} %hid_hbm.1, s32[8,128]{1,0:T(8,128)} %bitcast.7, s32[1,17]{1,0:T(1,128)} %rb_hbm.1, ...), custom_call_target="tpu_custom_call" | custom-call | tf_op jit(solution)/shard_map/score_gather_head/pallas_call | solution.py:385
  44.9 8.0 %bin_mix.1 = f32[32,8192]{1,0:T(8,128)} custom-call(s32[18432]{0:T(1024)} %bitcast.6, f32[16,272,128]{2,1,0:T(8,128)} %get-tuple-element.11.gath_hbm, f32[32,8192]{1,0:T(8,128)} %get-tuple-element.12.logit_hbm, f32[16,128]{1,0:T(8,128)} %get-tuple-element.13.scale_hbm, f32[64,128]{1,0:T(8,128)} %get-tuple-element.14.stat_hbm), custom_call_target="tpu_custom_call" | custom-call | tf_op jit(solution)/shard_map/bin_mix/pallas_call | solution.py:427
